TPU v7x, 128 devices: a whole 4x4x4 slice. The times are simulated.
128 devices in a mesh: seq: 64 (over y, z, x_lo, core), head: 2 (over x_hi).
Axes of the slice: x: 4 (x_hi: 2, x_lo: 2; x = x_hi * 2 + x_lo), y: 4, z: 4, core: 2. Of those that a mesh axis runs over, the one named last changes fastest.
Arguments:
- tokens: bfloat16 [32768, 2048], P('seq', 'head'), may hold values from -200 to 200
- norm_gain: float32 [2, 2048], replicated, may hold values from 0.25 to 1.75
- w_query: bfloat16 [2, 2048, 2048], P(None, None, 'head'), may hold values from -0.35 to 0.35
- key_projection_weight: bfloat16 [2, 2048, 512], P(None, None, 'head'), may hold values from -0.35 to 0.35
- value_projection_weight: bfloat16 [2, 2048, 512], P(None, None, 'head'), may hold values from -0.125 to 0.125
- w_out: bfloat16 [2, 2048, 2048], P(None, 'head'), may hold values from -0.125 to 0.125
- counts: int32 [64], replicated, may hold values from 128 to 512
Outputs:
- hidden_out: bfloat16 [32768, 2048], P('seq', 'head')
Inputs may be any that keep to these rules, and one draw needn't show every extreme that they name: The first counts[b] tokens of block b of 512 positions are valid keys; the rest of the block is padding that no query uses as a key.
All inputs are finite; a program needn't handle non-finite values.
Results may differ from a plain program's by a relative error of at most 0.02.
The roundings to bfloat16 on the way count: a program that leaves them out, or rounds other values in their place, can miss the bound.
Values may be sent and summed in bfloat16 or wider, within the bound.
A program may use at most 128 MiB of HBM per device.

v0:
```python
import math

import jax
import jax.numpy as jnp
from jax import lax
from jax.sharding import PartitionSpec as P

MODEL_WIDTH = 2048
HEAD_SIZE = 128
WINDOW = 4096
LAYER_COUNT = 2


norm_epsilon = 1e-05
rope_base = 10000.0


def passed_along(value, axis, steps):
    count = lax.axis_size(axis)
    initial, last = (max(0, -steps), min(count, count - steps))
    return lax.ppermute(value, axis, [(source, source + steps) for source in range(initial, last)])


def over_pieces(shard, axis):
    return lax.all_gather(shard, axis).sum(0)


def cut_along(shard, dim, length):
    shape = shard.shape
    blocks = shard.reshape(*shape[:dim], length, shape[dim] // length, *shape[dim + 1 :])
    return jnp.moveaxis(blocks, dim, 0)


def sum_at_owner(shard, axis, dim):
    blocks = cut_along(shard, dim, lax.axis_size(axis))
    arrived = lax.all_to_all(blocks, axis, split_axis=0, concat_axis=0, tiled=True)
    return arrived.astype(jnp.float32).sum(axis=0)


def rotate_heads(projected, token_positions, head_count):
    row_total = projected.shape[0]
    shaped = projected.reshape(row_total, head_count, HEAD_SIZE)
    half_dim = HEAD_SIZE // 2
    inverse = jnp.power(
        jnp.float32(rope_base), -2.0 * jnp.arange(half_dim, dtype=jnp.float32) / HEAD_SIZE
    )
    angles = token_positions.astype(jnp.float32)[:, None] * inverse[None, :]
    cosine_table = jnp.cos(angles)[:, None, :]
    sine_table = jnp.sin(angles)[:, None, :]
    first_half = shaped[..., :half_dim]
    second_half = shaped[..., half_dim:]
    rotated = jnp.concatenate(
        [
            first_half * cosine_table - second_half * sine_table,
            second_half * cosine_table + first_half * sine_table,
        ],
        axis=-1,
    )
    return rotated.astype(jnp.bfloat16)


def block_mask(counts, block_index, rows_here, span_blocks):
    key_length = (span_blocks + 1) * rows_here
    first_row = block_index * rows_here
    query_positions = first_row + jnp.arange(rows_here, dtype=jnp.int32)
    key_positions = first_row - span_blocks * rows_here + jnp.arange(key_length, dtype=jnp.int32)
    block_numbers = block_index - span_blocks + jnp.arange(span_blocks + 1, dtype=jnp.int32)
    table_size = counts.shape[0]
    matches = block_numbers[:, None] == jnp.arange(table_size, dtype=jnp.int32)[None, :]
    block_counts = jnp.sum(jnp.where(matches, counts[None, :], 0), axis=1)
    within_block = jnp.arange(rows_here, dtype=jnp.int32)
    valid_keys = (
        (block_numbers[:, None] >= 0) & (within_block[None, :] < block_counts[:, None])
    ).reshape(key_length)
    allowed = valid_keys[None, :] & (key_positions[None, :] <= query_positions[:, None])
    return allowed & (query_positions[:, None] - key_positions[None, :] < WINDOW)


def attend_local(queries, stacked, allowed):
    rows_here = queries.shape[0]
    local_heads = queries.shape[1]
    block_total = stacked.shape[0]
    local_groups = stacked.shape[3] // HEAD_SIZE
    key_length = block_total * rows_here
    key_heads = stacked[:, 0].reshape(key_length, local_groups, HEAD_SIZE).transpose(1, 0, 2)
    value_heads = stacked[:, 1].reshape(key_length, local_groups, HEAD_SIZE).transpose(1, 0, 2)
    query_heads = queries.transpose(1, 0, 2)
    group_length = local_heads // local_groups
    scale_factor = 1.0 / math.sqrt(HEAD_SIZE)

    def one_head(head_number):
        query_one = lax.dynamic_index_in_dim(query_heads, head_number, 0, keepdims=False)
        key_one = lax.dynamic_index_in_dim(
            key_heads, head_number // group_length, 0, keepdims=False
        )
        value_one = lax.dynamic_index_in_dim(
            value_heads, head_number // group_length, 0, keepdims=False
        )
        scores = (
            lax.dot_general(
                query_one, key_one, (((1,), (1,)), ((), ())), preferred_element_type=jnp.float32
            )
            * scale_factor
        )
        scores = jnp.where(allowed, scores, -jnp.inf)
        largest = jnp.max(scores, axis=1, keepdims=True)
        weights = jnp.exp(scores - largest)
        weights = (weights / jnp.sum(weights, axis=1, keepdims=True)).astype(jnp.bfloat16)
        return jnp.dot(weights, value_one, preferred_element_type=jnp.float32).astype(jnp.bfloat16)

    blended = lax.map(one_head, jnp.arange(local_heads, dtype=jnp.int32))
    return blended.transpose(1, 0, 2).reshape(rows_here, local_heads * HEAD_SIZE)


def doubling_blocks(stacked_own, span_blocks):
    gathered = stacked_own[None]
    have_blocks = 1
    while have_blocks < span_blocks + 1:
        needed = min(have_blocks, span_blocks + 1 - have_blocks)
        arrived = passed_along(gathered[have_blocks - needed :], "seq", have_blocks)
        gathered = jnp.concatenate([arrived, gathered], axis=0)
        have_blocks = have_blocks + needed
    return gathered


def per_device(
    tokens, norm_gain, w_query, key_projection_weight, value_projection_weight, w_out, counts
):
    rows_here = tokens.shape[0]
    half_width = tokens.shape[1]
    span_blocks = WINDOW // rows_here
    block_index = lax.axis_index("seq")
    head_index = lax.axis_index("head")
    token_positions = block_index * rows_here + jnp.arange(rows_here, dtype=jnp.int32)
    allowed = block_mask(counts, block_index, rows_here, span_blocks)
    local_query = w_query.shape[2] // HEAD_SIZE
    local_kv = key_projection_weight.shape[2] // HEAD_SIZE
    hidden = tokens
    for layer_position in range(LAYER_COUNT):
        gain_row = norm_gain[layer_position]
        query_weight = w_query[layer_position]
        key_weight = key_projection_weight[layer_position]
        value_weight = value_projection_weight[layer_position]
        widened = hidden.astype(jnp.float32)
        total_squares = over_pieces(jnp.sum(widened * widened, axis=1), "head")
        gain_part = lax.dynamic_slice_in_dim(gain_row, head_index * half_width, half_width, 0)
        normed_part = (
            widened
            * lax.rsqrt(total_squares / MODEL_WIDTH + norm_epsilon)[:, None]
            * gain_part[None, :]
        ).astype(jnp.bfloat16)

        def project_piece(
            running, piece_rows, offset, weights_now=(query_weight, key_weight, value_weight)
        ):
            width_here = piece_rows.shape[1]
            return tuple(
                (
                    jnp.dot(piece_rows, weight, preferred_element_type=jnp.float32)
                    for weight in weights_now
                )
            )

        starting = (
            jnp.zeros((rows_here, query_weight.shape[1]), jnp.float32),
            jnp.zeros((rows_here, key_weight.shape[1]), jnp.float32),
            jnp.zeros((rows_here, value_weight.shape[1]), jnp.float32),
        )
        query_raw, key_raw, value_raw = project_piece(
            starting, lax.all_gather(normed_part, "head", axis=1, tiled=True), jnp.int32(0)
        )
        queries = rotate_heads(query_raw, token_positions, local_query)
        keys_own = rotate_heads(key_raw, token_positions, local_kv).reshape(
            rows_here, local_kv * HEAD_SIZE
        )
        values_own = value_raw.astype(jnp.bfloat16)
        stacked_own = jnp.stack([keys_own, values_own])
        stacked = doubling_blocks(stacked_own, span_blocks)
        attended = attend_local(queries, stacked, allowed)
        partial_product = jnp.dot(
            attended, w_out[layer_position], preferred_element_type=jnp.float32
        )
        rounded = lax.optimization_barrier(partial_product.astype(jnp.bfloat16)).astype(jnp.float32)
        own_share = sum_at_owner(rounded.astype(jnp.bfloat16), "head", 1)
        hidden = (hidden.astype(jnp.float32) + own_share).astype(jnp.bfloat16)
    return hidden


def solution(mesh):
    return jax.shard_map(
        per_device,
        mesh=mesh,
        in_specs=(
            P("seq", "head"),
            P(),
            P(None, None, "head"),
            P(None, None, "head"),
            P(None, None, "head"),
            P(None, "head", None),
            P(),
        ),
        out_specs=P("seq", "head"),
        check_vma=False,
    )
```

profile of v0, /device:TPU:42, one launch (start us, length us, event | category | flops | bytes accessed | tf_op | source)
XLA Modules:
  0.0 660.5 jit_solution(10154303628306958969)
XLA Ops:
  8.9 5.9 all-gather.2
  19.7 35.9 %all-gather.7.cloned.1.call-done = bf16[512,2048]{1,0:T(8,128)(2,1)} async-done(((bf16[512,1024]{1,0:T(8,128)(2,1)}), bf16[512,2048]{1,0:T(8,128)(2,1)}) %all-gather.7.cloned.1.call-update) | async-done | bytes 2097168 | tf_op jit(solution)/shard_map/all_gather | solution.py:170
  62.8 8.6 %collective-permute-done.1 = bf16[1,2,512,256]{3,2,1,0:T(8,128)(2,1)S(1)} collective-permute-done((bf16[1,2,512,256]{3,2,1,0:T(8,128)(2,1)S(1)}, bf16[1,2,512,256]{3,2,1,0:T(8,128)(2,1)S(1)}, u32[]{:S(2)}, u32[]{:S(2)}) %collective-permute-start.1) | collective-permute-done | bytes 524320 | tf_op jit(solution)/shard_map/ppermute | solution.py:21
  76.8 21.8 %collective-permute-done.2 = bf16[2,2,512,256]{3,2,1,0:T(8,128)(2,1)S(1)} collective-permute-done((bf16[2,2,512,256]{3,2,1,0:T(8,128)(2,1)S(1)}, bf16[2,2,512,256]{3,2,1,0:T(8,128)(2,1)S(1)}, u32[]{:S(2)}, u32[]{:S(2)}) %collective-permute-start.2) | collective-permute-done | bytes 1048608 | tf_op jit(solution)/shard_map/ppermute | solution.py:21
  103.2 5.9 slice_bitcast_fusion.1
  109.1 6.5 copy.50
  126.7 44.1 %collective-permute-done = bf16[1,2,512,256]{3,2,1,0:T(8,128)(2,1)S(1)} collective-permute-done((bf16[1,2,512,256]{3,2,1,0:T(8,128)(2,1)S(1)}, bf16[1,2,512,256]{3,2,1,0:T(8,128)(2,1)S(1)}, u32[]{:S(2)}, u32[]{:S(2)}) %collective-permute-start) | collective-permute-done | bytes 524320 | tf_op jit(solution)/shard_map/ppermute | solution.py:21
  189.3 113.2 %while.26 = (s32[]{:T(128)}, bf16[8,512,128]{1,2,0:T(8,128)(2,1)}, s32[8]{0:T(128)S(1)}, bf16[8,512,128]{1,2,0:T(8,128)(2,1)}, bf16[2,4608,128]{2,1,0:T(8,128)(2...) while((s32[]{:T(128)}, bf16[8,512,128]{1,2,0:T(8,128)(2,1)}, ...), condition=%wide.region_6.7_spmd.clone, body=%wide.region_3.6_spmd.clone.sunk | while | flops 1238694912 | bytes 40930704 | solution.py:111
  193.8 5.6 fusion.97
  207.9 5.6 fusion.97
  222.0 5.6 fusion.97
  236.1 5.6 fusion.97
  250.2 5.6 fusion.97
  264.4 5.6 fusion.97
  278.5 5.6 fusion.97
  292.6 5.6 fusion.97
  312.8 23.1 %all-to-all-done = bf16[2,512,1024]{2,1,0:T(8,128)(2,1)S(1)} async-done(((bf16[2,512,1024]{2,1,0:T(8,128)(2,1)}), bf16[2,512,1024]{2,1,0:T(8,128)(2,1)S(1)}, u32[]{:S(2)}, u32[]{:S(2)}) %all-to-all-start) | async-done | bytes 2097184 | tf_op jit(solution)/shard_map/all_to_all | solution.py:36
  336.7 6.0 all-gather.3
  344.7 33.9 %all-gather.9.cloned.1.call-done = bf16[512,2048]{1,0:T(8,128)(2,1)} async-done(((bf16[512,1024]{1,0:T(8,128)(2,1)}), bf16[512,2048]{1,0:T(8,128)(2,1)}) %all-gather.9.cloned.1.call-update) | async-done | bytes 2097168 | tf_op jit(solution)/shard_map/all_gather | solution.py:170
  386.6 8.6 %collective-permute-done.5 = bf16[1,2,512,256]{3,2,1,0:T(8,128)(2,1)S(1)} collective-permute-done((bf16[1,2,512,256]{3,2,1,0:T(8,128)(2,1)S(1)}, bf16[1,2,512,256]{3,2,1,0:T(8,128)(2,1)S(1)}, u32[]{:S(2)}, u32[]{:S(2)}) %collective-permute-start.5) | collective-permute-done | bytes 524320 | tf_op jit(solution)/shard_map/ppermute | solution.py:21
  400.6 21.8 %collective-permute-done.6 = bf16[2,2,512,256]{3,2,1,0:T(8,128)(2,1)S(1)} collective-permute-done((bf16[2,2,512,256]{3,2,1,0:T(8,128)(2,1)S(1)}, bf16[2,2,512,256]{3,2,1,0:T(8,128)(2,1)S(1)}, u32[]{:S(2)}, u32[]{:S(2)}) %collective-permute-start.6) | collective-permute-done | bytes 1048608 | tf_op jit(solution)/shard_map/ppermute | solution.py:21
  427.1 6.5 copy.58
  444.3 50.3 %collective-permute-done.4 = bf16[1,2,512,256]{3,2,1,0:T(8,128)(2,1)S(1)} collective-permute-done((bf16[1,2,512,256]{3,2,1,0:T(8,128)(2,1)S(1)}, bf16[1,2,512,256]{3,2,1,0:T(8,128)(2,1)S(1)}, u32[]{:S(2)}, u32[]{:S(2)}) %collective-permute-start.4) | collective-permute-done | bytes 524320 | tf_op jit(solution)/shard_map/ppermute | solution.py:21
  513.0 107.8 %while.27 = (s32[]{:T(128)}, bf16[8,512,128]{1,2,0:T(8,128)(2,1)S(1)}, s32[8]{0:T(128)S(1)}, bf16[8,512,128]{1,2,0:T(8,128)(2,1)}, bf16[2,4608,128]{2,1,0:T(8,12...) while((s32[]{:T(128)}, ...), condition=%wide.region_13.14_spmd.clone, body=%wide.region_10.13_spmd.clone.sunk | while | flops 1238694912 | bytes 40930196 | solution.py:111
  517.5 5.6 fusion.101
  530.9 5.6 fusion.101
  544.3 5.6 fusion.101
  557.8 5.6 fusion.101
  571.2 5.6 fusion.101
  598.1 5.6 fusion.101
  611.5 5.6 fusion.101
  625.5 25.8 %all_to_all.10 = bf16[2,512,1024]{2,1,0:T(8,128)(2,1)S(1)} all-to-all(bf16[2,512,1024]{2,1,0:T(8,128)(2,1)S(1)} %bitcast.179), channel_id=1, replica_groups=mesh['seq'=64,'head'=2] {'head'}, dimensions={0} | all-to-all | bytes 4194304 | tf_op jit(solution)/shard_map/all_to_all | solution.py:36
  (228 shorter events, 195.7 us)
Async XLA Ops:
  6.5 10.9 %copy-start.8 = (bf16[2,2048,256]{2,1,0:T(8,128)(2,1)S(1)}, bf16[2,2048,256]{2,1,0:T(8,128)(2,1)}, u32[]{:S(2)}) copy-start(bf16[2,2048,256]{2,1,0:T(8,128)(2,1)} %param.14) | copy-start | bytes 6291460
  6.5 49.1 %all-gather.7.cloned.1.call-start = ((), (), s32[]{:S(2)}) async-start(), calls=%async_computation.2 | async-start | bytes 3145728 | tf_op jit(solution)/shard_map/all_gather | solution.py:170
  19.7 105.6 %copy-start.2 = (f32[512,64]{0,1:T(8,128)}, f32[512,64]{0,1:T(8,128)S(1)}, u32[]{:S(2)}) copy-start(f32[512,64]{0,1:T(8,128)S(1)} %get-tuple-element.366) | copy-start | bytes 393220
  60.9 10.5 %collective-permute-start.1 = (bf16[1,2,512,256]{3,2,1,0:T(8,128)(2,1)S(1)}, bf16[1,2,512,256]{3,2,1,0:T(8,128)(2,1)S(1)}, u32[]{:S(2)}, u32[]{:S(2)}) collective-permute-start(bf16[1,2,512,256]{3,2,1,0:T(8,128)(2,1)S(1)} %maximum_bitcast_fusion.2), channel_id=1, source_target_pairs={{0,2},{2,4},{4,6},{6,8},{8,10},{10,12},{12,14},{14,16},{16,18},{18... | collective-permute-start | bytes 1572872 | tf_op jit(solution)/shard_map/ppermute | solution.py:21
  71.5 27.0 %collective-permute-start.2 = (bf16[2,2,512,256]{3,2,1,0:T(8,128)(2,1)S(1)}, bf16[2,2,512,256]{3,2,1,0:T(8,128)(2,1)S(1)}, u32[]{:S(2)}, u32[]{:S(2)}) collective-permute-start(bf16[2,2,512,256]{3,2,1,0:T(8,128)(2,1)S(1)} %pad_maximum_fusion.2), channel_id=1, source_target_pairs={{0,4},{2,6},{4,8},{6,10},{8,12},{10,14},{12,16},{14,18},{16,20},{1... | collective-permute-start | bytes 3145736 | tf_op jit(solution)/shard_map/ppermute | solution.py:21
  100.1 70.8 %collective-permute-start.3 = (bf16[4,2,512,256]{3,2,1,0:T(8,128)(2,1)}, bf16[4,2,512,256]{3,2,1,0:T(8,128)(2,1)}, u32[]{:S(2)}, u32[]{:S(2)}) collective-permute-start(bf16[4,2,512,256]{3,2,1,0:T(8,128)(2,1)} %pad_maximum_fusion), channel_id=1, source_target_pairs={{0,8},{2,10},{4,12},{6,14},{8,16},{10,18},{12,20},{14,22},{16,24},... | collective-permute-start | bytes 6291464 | tf_op jit(solution)/shard_map/ppermute | solution.py:21
  109.1 6.5 copy-start.13
  116.0 54.8 %collective-permute-start = (bf16[1,2,512,256]{3,2,1,0:T(8,128)(2,1)S(1)}, bf16[1,2,512,256]{3,2,1,0:T(8,128)(2,1)S(1)}, u32[]{:S(2)}, u32[]{:S(2)}) collective-permute-start(bf16[1,2,512,256]{3,2,1,0:T(8,128)(2,1)S(1)} %maximum_bitcast_fusion.2), channel_id=1, source_target_pairs={{0,16},{2,18},{4,20},{6,22},{8,24},{10,26},{12,28},{14,30},{16,32}... | collective-permute-start | bytes 1572872 | tf_op jit(solution)/shard_map/ppermute | solution.py:21
  199.3 1.7 copy-start.5
  213.5 1.7 copy-start.5
  227.6 1.7 copy-start.5
  241.7 1.7 copy-start.5
  255.8 1.7 copy-start.5
  269.9 1.7 copy-start.5
  284.1 1.7 copy-start.5
  298.2 1.7 copy-start.5
  302.5 4.9 copy-start.11
  308.9 26.9 %all-to-all-start = ((bf16[2,512,1024]{2,1,0:T(8,128)(2,1)}), bf16[2,512,1024]{2,1,0:T(8,128)(2,1)S(1)}, u32[]{:S(2)}, u32[]{:S(2)}) async-start(bf16[2,512,1024]{2,1,0:T(8,128)(2,1)} %bitcast.178), calls=%async_computation | async-start | bytes 4194304 | tf_op jit(solution)/shard_map/all_to_all | solution.py:36
  312.7 23.6 %copy-start = (bf16[512,1024]{1,0:T(8,128)(2,1)S(1)}, bf16[512,1024]{1,0:T(8,128)(2,1)}, u32[]{:S(2)}) copy-start(bf16[512,1024]{1,0:T(8,128)(2,1)} %param.11) | copy-start | bytes 3145732
  312.7 65.9 %all-gather.9.cloned.1.call-start = ((), (), s32[]{:S(2)}) async-start(), calls=%async_computation.3 | async-start | bytes 3145728 | tf_op jit(solution)/shard_map/all_gather | solution.py:170
  336.7 7.4 %copy-start.1 = (bf16[256,2048]{0,1:T(8,128)(2,1)S(1)}, bf16[256,2048]{0,1:T(8,128)(2,1)}, u32[]{:S(2)}) copy-start(bf16[256,2048]{0,1:T(8,128)(2,1)} %get-tuple-element.357) | copy-start | bytes 3145732
  378.6 2.4 copy-start.3
  381.3 2.7 copy-start.6
  384.7 10.5 %collective-permute-start.5 = (bf16[1,2,512,256]{3,2,1,0:T(8,128)(2,1)S(1)}, bf16[1,2,512,256]{3,2,1,0:T(8,128)(2,1)S(1)}, u32[]{:S(2)}, u32[]{:S(2)}) collective-permute-start(bf16[1,2,512,256]{3,2,1,0:T(8,128)(2,1)S(1)} %maximum_bitcast_fusion.3), channel_id=1, source_target_pairs={{0,2},{2,4},{4,6},{6,8},{8,10},{10,12},{12,14},{14,16},{16,18},{18... | collective-permute-start | bytes 1572872 | tf_op jit(solution)/shard_map/ppermute | solution.py:21
  395.3 27.0 %collective-permute-start.6 = (bf16[2,2,512,256]{3,2,1,0:T(8,128)(2,1)S(1)}, bf16[2,2,512,256]{3,2,1,0:T(8,128)(2,1)S(1)}, u32[]{:S(2)}, u32[]{:S(2)}) collective-permute-start(bf16[2,2,512,256]{3,2,1,0:T(8,128)(2,1)S(1)} %pad_maximum_fusion.3), channel_id=1, source_target_pairs={{0,4},{2,6},{4,8},{6,10},{8,12},{10,14},{12,16},{14,18},{16,20},{1... | collective-permute-start | bytes 3145736 | tf_op jit(solution)/shard_map/ppermute | solution.py:21
  423.9 70.8 %collective-permute-start.7 = (bf16[4,2,512,256]{3,2,1,0:T(8,128)(2,1)}, bf16[4,2,512,256]{3,2,1,0:T(8,128)(2,1)}, u32[]{:S(2)}, u32[]{:S(2)}) collective-permute-start(bf16[4,2,512,256]{3,2,1,0:T(8,128)(2,1)} %pad_maximum_fusion.1), channel_id=1, source_target_pairs={{0,8},{2,10},{4,12},{6,14},{8,16},{10,18},{12,20},{14,22},{16,24},... | collective-permute-start | bytes 6291464 | tf_op jit(solution)/shard_map/ppermute | solution.py:21
  433.6 61.1 %collective-permute-start.4 = (bf16[1,2,512,256]{3,2,1,0:T(8,128)(2,1)S(1)}, bf16[1,2,512,256]{3,2,1,0:T(8,128)(2,1)S(1)}, u32[]{:S(2)}, u32[]{:S(2)}) collective-permute-start(bf16[1,2,512,256]{3,2,1,0:T(8,128)(2,1)S(1)} %maximum_bitcast_fusion.3), channel_id=1, source_target_pairs={{0,16},{2,18},{4,20},{6,22},{8,24},{10,26},{12,28},{14,30},{16,32}... | collective-permute-start | bytes 1572872 | tf_op jit(solution)/shard_map/ppermute | solution.py:21
  511.2 1.8 copy-start.12
  523.1 1.7 copy-start.4
  549.9 1.7 copy-start.4
  590.2 1.7 copy-start.4
  617.1 1.7 copy-start.4
  (7 other events, 9.4 us)
Sparse Core Ops, SparseCore 0:
  17.5 38.1 all-gather.6
  344.2 34.3 all-gather.8
where the time goes:
time: 670 us; the launch traced here: 660 us
  waiting for transfers between devices  248 us (37%)
  matrix products  145 us (22%)
  local copies, waits for them, and re-layouts  83.2 us (12%)
  loops' own time  62.1 us (9%)
  other arithmetic  37.9 us (6%)
  blocking collectives  37.6 us (6%)
  starting transfers between devices  32.7 us (5%)
  between operations  14.5 us (2%)
    ppermute x8, waiting for transfers between devices, passed_along(): lax.ppermute(value, axis, [(source, source + steps) for source in range(i...  155 us
    dot_general x16, matrix products, one_head(): lax.dot_general(query_one, key_one, (((1,), (1,)), ((), ())), preferred_e...  89.2 us
    all_gather x2, waiting for transfers between devices, per_device(): lax.all_gather(normed_part, 'head', axis=1, tiled=True)  69.8 us
    another operation x2, loops' own time, attend_local(): blended = lax.map(one_head, jnp.arange(local_heads, dtype=jnp.int32))  62.1 us
    ppermute x8, starting transfers between devices, passed_along(): lax.ppermute(value, axis, [(source, source + steps) for source in range(i...  28.9 us
    all_to_all x1, blocking collectives, sum_at_owner(): lax.all_to_all(blocks, axis, split_axis=0, concat_axis=0, tiled=True)  25.8 us
    dot_general x16, matrix products, one_head(): jnp.dot(weights, value_one, preferred_element_type=jnp.float32)  25.6 us
    all_to_all x1, waiting for transfers between devices, sum_at_owner(): lax.all_to_all(blocks, axis, split_axis=0, concat_axis=0, tiled=True)  23.1 us
  transfers between devices with their start and end apart: 11, of which 9 were waited for; matrix products, arithmetic and copies ran while one was open for 5% of the time, Pallas kernels for 0%

commit v1 on v0

v1 whole, which is shorter than its diff:
```python
import functools
import math

import jax
import jax.numpy as jnp
from jax import lax
from jax.experimental import pallas as pl
from jax.experimental.pallas import tpu as pltpu
from jax.sharding import PartitionSpec as P

MODEL_WIDTH = 2048
HEAD_SIZE = 128
WINDOW = 4096
LAYER_COUNT = 2
ROWS = 512
HALF = 1024
CHUNK = 128
CHUNKS = 4
SLOTS = 9
NORM_EPSILON = 1e-05
ROPE_BASE = 10000.0
LOW = -1e30
QUERY_SCALE = math.log2(math.e) / math.sqrt(HEAD_SIZE)
NT = (((1,), (1,)), ((), ()))


def mega(
    blocks,
    tok, gain, wq, wk, wv, wo, cos_ref, sin_ref, counts, out_ref,
    xb, wqb, wkvb, wob, nb, qs, kv, vm, m_ref, acc, ab, pb, pr, pb1, pr1,
    ld_sem, ts, tr, zs, zr, xs, xr, os_, or_, cs, cr, ps, pr_sem,
):
    seq = lax.axis_index("seq")
    head = lax.axis_index("head")
    core = lax.rem(seq, 2)
    xlo = lax.rem(lax.div(seq, 2), 2)
    nxt = lax.rem(seq + 4, blocks)
    prv = lax.rem(seq + blocks - 4, blocks)
    xpeer = seq + 2 - 4 * xlo
    cpeer = seq + 1 - 2 * core
    pair = 1 - head
    mesh_id = pl.DeviceIdType.MESH

    def local(src, dst, n):
        return pltpu.make_async_copy(src, dst, ld_sem.at[n])

    loads = [local(tok, xb.at[head], 0)]
    for l in range(LAYER_COUNT):
        loads.append(local(wk.at[l], wkvb.at[l, :, 0:256], 4 * l + 1))
        loads.append(local(wv.at[l], wkvb.at[l, :, 256:512], 4 * l + 2))
        loads.append(local(wq.at[l], wqb.at[l], 4 * l + 3))
        loads.append(local(wo.at[l], wob.at[l], 4 * l + 4))

    barrier = pltpu.get_barrier_semaphore()
    for target in (
        {"seq": prv, "head": head},
        {"seq": xpeer, "head": head},
        {"seq": cpeer, "head": head},
        {"seq": seq, "head": pair},
    ):
        pl.semaphore_signal(barrier, inc=1, device_id=target, device_id_type=mesh_id)
    for load in loads:
        load.start()
    pl.semaphore_wait(barrier, 4)

    def rc_rows(c):
        return pl.ds(c * CHUNK, CHUNK)

    def tok_copy(c):
        return pltpu.make_async_remote_copy(
            src_ref=tok.at[rc_rows(c), :], dst_ref=xb.at[head, rc_rows(c), :],
            send_sem=ts.at[c], recv_sem=tr.at[c],
            device_id={"seq": seq, "head": pair}, device_id_type=mesh_id)

    for c in range(CHUNKS):
        tok_copy(c).start()

    def kv_copy(l, c, src_slot, dst_slot, send, recv, stage, target):
        return pltpu.make_async_remote_copy(
            src_ref=kv.at[l, src_slot, c], dst_ref=kv.at[l, dst_slot, c],
            send_sem=send.at[l, stage, c], recv_sem=recv.at[l, stage, c],
            device_id={"seq": target, "head": head}, device_id_type=mesh_id)

    def z_copy(l, c, i):
        return kv_copy(l, c, 4 * i, 4 * i + 4, zs, zr, i, nxt)

    def x_copy(l, c, i):
        return kv_copy(l, c, 4 * i + 4 * xlo, 4 * i + 2, xs, xr, i, xpeer)

    def o_copy(l, c, i):
        return kv_copy(l, c, 4 * i + 4 * core, 4 * i + 1 + 2 * core, os_, or_, i, cpeer)

    def c_copy(l, c, i):
        return kv_copy(l, c, 4 * i + 2, 4 * i + 3 - 2 * core, cs, cr, i, cpeer)

    def event0(l, c):
        z_copy(l, c, 0).start()

        @pl.when(xlo == 0)
        def _():
            x_copy(l, c, 0).start()

        @pl.when(core == 0)
        def _():
            o_copy(l, c, 0).start()

    def event1(l, c):
        z_copy(l, c, 0).wait_recv()
        z_copy(l, c, 1).start()

        @pl.when(xlo == 1)
        def _():
            x_copy(l, c, 0).start()

        @pl.when(xlo == 0)
        def _():
            x_copy(l, c, 1).start()

        @pl.when(core == 1)
        def _():
            o_copy(l, c, 0).start()

        @pl.when(core == 0)
        def _():
            o_copy(l, c, 1).start()

    def event2(l, c):
        x_copy(l, c, 0).wait_recv()
        c_copy(l, c, 0).start()

    def event3(l, c):
        z_copy(l, c, 1).wait_recv()

        @pl.when(xlo == 1)
        def _():
            x_copy(l, c, 1).start()

        @pl.when(core == 1)
        def _():
            o_copy(l, c, 1).start()

    def event4(l, c):
        x_copy(l, c, 1).wait_recv()
        c_copy(l, c, 1).start()

    own_count = counts[seq]
    lanes = lax.broadcasted_iota(jnp.int32, (16, ROWS), 1)
    sub = lax.broadcasted_iota(jnp.int32, (16, ROWS), 0)
    for d in range(SLOTS):
        n_valid = counts[lax.rem(seq + blocks - d, blocks)]
        vm[d] = jnp.where((lanes < n_valid) & (sub == 0), 1.0, 0.0).astype(jnp.bfloat16)
    far_count = counts[lax.rem(seq + blocks - 8, blocks)]

    def rope(val, cos, sin):
        return val * cos + pltpu.roll(val, 64, 1) * sin

    def project(l, c):
        rows = rc_rows(c)
        x0 = xb[0, rows, :].astype(jnp.float32)
        x1 = xb[1, rows, :].astype(jnp.float32)
        total = jnp.sum(x0 * x0, axis=1, keepdims=True) + jnp.sum(x1 * x1, axis=1, keepdims=True)
        factor = lax.rsqrt(total / MODEL_WIDTH + NORM_EPSILON)
        nb[:, 0:HALF] = (x0 * factor * gain[l : l + 1, 0:HALF]).astype(jnp.bfloat16)
        nb[:, HALF:] = (x1 * factor * gain[l : l + 1, HALF:]).astype(jnp.bfloat16)
        cos = cos_ref[rows, :]
        sin = sin_ref[rows, :]
        kvp = jnp.dot(nb[...], wkvb[l], preferred_element_type=jnp.float32)
        valid = lax.broadcasted_iota(jnp.int32, (CHUNK, HEAD_SIZE), 0) + c * CHUNK < own_count
        for g in range(2):
            key = rope(kvp[:, g * 128 : (g + 1) * 128], cos, sin).astype(jnp.bfloat16)
            if c > 0:
                first = kv[l, 0, 0, g * 128 : g * 128 + 1, :]
                key = jnp.where(valid, key.astype(jnp.float32), first.astype(jnp.float32)).astype(jnp.bfloat16)
            kv[l, 0, c, g * 128 : (g + 1) * 128, :] = key
            val = jnp.where(valid, kvp[:, 256 + g * 128 : 256 + (g + 1) * 128], 0.0)
            kv[l, 0, c, 256 + g * 128 : 256 + (g + 1) * 128, :] = val.T.astype(jnp.bfloat16)
        event0(l, c)
        for half in range(2):
            qp = jnp.dot(nb[...], wqb[l, :, half * 512 : (half + 1) * 512], preferred_element_type=jnp.float32)
            for h in range(4):
                rot = rope(qp[:, h * 128 : (h + 1) * 128], cos, sin) * QUERY_SCALE
                qs[half * 4 + c, h * 128 : (h + 1) * 128, :] = rot.astype(jnp.bfloat16)

    def keys_of(l, slot, g, lo, hi):
        return jnp.concatenate([kv[l, slot, c, g * 128 : (g + 1) * 128, :] for c in range(lo, hi)], axis=0)

    def values_of(l, slot, g, lo, hi):
        vt = jnp.concatenate([kv[l, slot, c, 256 + g * 128 : 256 + (g + 1) * 128, :] for c in range(lo, hi)], axis=1)
        return jnp.concatenate([vt, vm[slot, :, lo * 128 : hi * 128]], axis=0)

    units = [(g, c) for g in range(2) for c in range(CHUNKS)]

    def scores(l, slot, g, c, lo, hi):
        return lax.dot_general(keys_of(l, slot, g, lo, hi), qs[g * 4 + c], NT, preferred_element_type=jnp.float32)

    def sweep(l, slot, bounds, mask, first):
        nxt_s = scores(l, slot, *units[0], *bounds(units[0][1]))
        for n, (g, c) in enumerate(units):
            s = nxt_s
            if n + 1 < len(units):
                nxt_s = scores(l, slot, *units[n + 1], *bounds(units[n + 1][1]))
            lo, hi = bounds(c)
            u = g * 4 + c
            if mask is not None:
                key_at = lax.broadcasted_iota(jnp.int32, s.shape, 0) + lo * 128
                row_at = (lax.broadcasted_iota(jnp.int32, s.shape, 1) & 127) + c * CHUNK
                s = jnp.where(mask(key_at, row_at), s, LOW)
            top = jnp.max(s, axis=0, keepdims=True)
            if first:
                m_new = top
            else:
                m_old = m_ref[u]
                m_new = jnp.maximum(m_old, top)
            p = jnp.exp2(s - m_new).astype(jnp.bfloat16)
            part = jnp.dot(values_of(l, slot, g, lo, hi), p, preferred_element_type=jnp.float32)
            m_ref[u] = m_new
            if first:
                acc[u] = part
            else:
                acc[u] = acc[u] * jnp.exp2(m_old - m_new) + part

    def attention(l):
        sweep(l, 0, lambda c: (0, c + 1), lambda key_at, row_at: key_at <= row_at, True)
        event1(l, 3)
        event2(l, 2)
        event3(l, 2)
        event4(l, 1)

        def step(n, carry):
            @pl.when(n == 1)
            def _():
                event2(l, 3)
                event3(l, 3)
                event4(l, 2)
                for c in range(CHUNKS):
                    o_copy(l, c, 0).wait_recv()

            @pl.when(n == 3)
            def _():
                event4(l, 3)
                for c in range(CHUNKS):
                    c_copy(l, c, 0).wait_recv()

                @pl.when(seq >= 8)
                def _():
                    sweep(l, 8, lambda c: (c, 4), lambda key_at, row_at: (key_at > row_at) & (key_at < far_count), False)

            @pl.when(n == 5)
            def _():
                for c in range(CHUNKS):
                    o_copy(l, c, 1).wait_recv()

            @pl.when(n == 6)
            def _():
                for c in range(CHUNKS):
                    c_copy(l, c, 1).wait_recv()

            sub_n = n % 4
            base = 4 * (n // 4)
            slot_lo = jnp.where(
                n == 0, 4, jnp.where(
                    n == 1, 3 - 2 * core, jnp.where(
                        n == 2, 2, jnp.where(
                            n == 3, 1 + 2 * core, jnp.where(
                                n == 4, 6, jnp.where(n == 5, 7 - 2 * core, 5 + 2 * core))))))

            @pl.when(seq >= slot_lo)
            def _():
                sweep(l, slot_lo, lambda c: (0, 4), None, False)

            return carry

        lax.fori_loop(0, 7, step, 0)

    def attended(c):
        for g in range(2):
            u = g * 4 + c
            norm = acc[u, 0:128, :] / acc[u, 128:129, :]
            for h in range(4):
                ab[:, (g * 4 + h) * 128 : (g * 4 + h + 1) * 128] = norm[:, h * 128 : (h + 1) * 128].T.astype(jnp.bfloat16)

    def full_copy(c):
        return pltpu.make_async_remote_copy(
            src_ref=pb.at[c], dst_ref=pr.at[c], send_sem=ps.at[0, c], recv_sem=pr_sem.at[0, c],
            device_id={"seq": seq, "head": pair}, device_id_type=mesh_id)

    def half_copy(c):
        return pltpu.make_async_remote_copy(
            src_ref=pb1.at[c], dst_ref=pr1.at[c], send_sem=ps.at[1, c], recv_sem=pr_sem.at[1, c],
            device_id={"seq": seq, "head": pair}, device_id_type=mesh_id)

    def early_events(l, c):
        if c >= 1:
            event1(l, c - 1)
        if c >= 2:
            event2(l, c - 2)
            event3(l, c - 2)
        if c >= 3:
            event4(l, c - 3)

    loads[0].wait()
    for c in range(CHUNKS):
        tok_copy(c).wait_recv()
        if c == 0:
            for load in loads[1:4]:
                load.wait()
        project(0, c)
        early_events(0, c)
    attention(0)
    loads[4].wait()
    for c in range(CHUNKS):
        attended(c)
        for half in range(2):
            pb[c, :, half * HALF : (half + 1) * HALF] = jnp.dot(
                ab[...], wob[0, :, half * HALF : (half + 1) * HALF], preferred_element_type=jnp.float32
            ).astype(jnp.bfloat16)
        full_copy(c).start()

    for load in loads[5:8]:
        load.wait()
    for c in range(CHUNKS):
        full_copy(c).wait_recv()
        rows = rc_rows(c)
        for half in range(2):
            cols = slice(half * HALF, (half + 1) * HALF)
            summed = pb[c, :, cols].astype(jnp.float32) + pr[c, :, cols].astype(jnp.float32)
            xb[half, rows, :] = (xb[half, rows, :].astype(jnp.float32) + summed).astype(jnp.bfloat16)
        project(1, c)
        early_events(1, c)
    attention(1)
    loads[8].wait()
    other_cols = pl.ds(pl.multiple_of(pair * HALF, HALF), HALF)
    own_cols = pl.ds(pl.multiple_of(head * HALF, HALF), HALF)
    for c in range(CHUNKS):
        rows = rc_rows(c)
        attended(c)
        pb1[c] = jnp.dot(ab[...], wob[1, :, other_cols], preferred_element_type=jnp.float32).astype(jnp.bfloat16)
        half_copy(c).start()
        out_ref[rows, :] = jnp.dot(ab[...], wob[1, :, own_cols], preferred_element_type=jnp.float32).astype(jnp.bfloat16)
    for c in range(CHUNKS):
        rows = rc_rows(c)
        half_copy(c).wait_recv()
        summed = out_ref[rows, :].astype(jnp.float32) + pr1[c].astype(jnp.float32)
        out_ref[rows, :] = (xb[head, rows, :].astype(jnp.float32) + summed).astype(jnp.bfloat16)

    for c in range(CHUNKS):
        tok_copy(c).wait_send()
        full_copy(c).wait_send()
        half_copy(c).wait_send()
        for l in range(LAYER_COUNT):
            for i in range(2):
                z_copy(l, c, i).wait_send()
                x_copy(l, c, i).wait_send()
                o_copy(l, c, i).wait_send()
                c_copy(l, c, i).wait_send()


def per_device(tokens, norm_gain, w_query, key_projection_weight, value_projection_weight, w_out, counts):
    blocks = lax.axis_size("seq")
    half_dim = HEAD_SIZE // 2
    positions = lax.axis_index("seq") * ROWS + jnp.arange(ROWS, dtype=jnp.int32)
    inverse = jnp.power(jnp.float32(ROPE_BASE), -2.0 * jnp.arange(half_dim, dtype=jnp.float32) / HEAD_SIZE)
    angles = positions.astype(jnp.float32)[:, None] * inverse[None, :]
    cosine, sine = jnp.cos(angles), jnp.sin(angles)
    cos2 = jnp.concatenate([cosine, cosine], axis=1)
    sin2 = jnp.concatenate([-sine, sine], axis=1)
    bf16, f32 = jnp.bfloat16, jnp.float32
    any_, vmem = pl.BlockSpec(memory_space=pl.ANY), pl.BlockSpec(memory_space=pltpu.VMEM)
    dma = pltpu.SemaphoreType.DMA
    return pl.pallas_call(
        functools.partial(mega, blocks),
        out_shape=jax.ShapeDtypeStruct((ROWS, HALF), bf16),
        in_specs=[any_, vmem, any_, any_, any_, any_, vmem, vmem, pl.BlockSpec(memory_space=pltpu.SMEM)],
        out_specs=vmem,
        scratch_shapes=[
            pltpu.VMEM((2, ROWS, HALF), bf16),
            pltpu.VMEM((2, MODEL_WIDTH, HALF), bf16),
            pltpu.VMEM((2, MODEL_WIDTH, 512), bf16),
            pltpu.VMEM((2, HALF, MODEL_WIDTH), bf16),
            pltpu.VMEM((CHUNK, MODEL_WIDTH), bf16),
            pltpu.VMEM((8, 512, 128), bf16),
            pltpu.VMEM((2, SLOTS, CHUNKS, 512, 128), bf16),
            pltpu.VMEM((SLOTS, 16, ROWS), bf16),
            pltpu.VMEM((8, 1, 512), f32),
            pltpu.VMEM((8, 144, 512), f32),
            pltpu.VMEM((CHUNK, HALF), bf16),
            pltpu.VMEM((CHUNKS, CHUNK, MODEL_WIDTH), bf16),
            pltpu.VMEM((CHUNKS, CHUNK, MODEL_WIDTH), bf16),
            pltpu.VMEM((CHUNKS, CHUNK, HALF), bf16),
            pltpu.VMEM((CHUNKS, CHUNK, HALF), bf16),
            dma((9,)), dma((4,)), dma((4,)),
            dma((2, 2, 4)), dma((2, 2, 4)), dma((2, 2, 4)), dma((2, 2, 4)),
            dma((2, 2, 4)), dma((2, 2, 4)), dma((2, 2, 4)), dma((2, 2, 4)),
            dma((2, 4)), dma((2, 4)),
        ],
        compiler_params=pltpu.CompilerParams(
            collective_id=0, has_side_effects=True, vmem_limit_bytes=63 * 2**20
        ),
    )(tokens, norm_gain, w_query, key_projection_weight, value_projection_weight, w_out, cos2, sin2, counts)


def solution(mesh):
    return jax.shard_map(
        per_device,
        mesh=mesh,
        in_specs=(
            P("seq", "head"),
            P(),
            P(None, None, "head"),
            P(None, None, "head"),
            P(None, None, "head"),
            P(None, "head", None),
            P(),
        ),
        out_specs=P("seq", "head"),
        check_vma=False,
    )
```

time: 670 us -> 186 us (0.28); the launches traced: 660 us -> 185 us
  waiting for transfers between devices: 248 us -> 0 us
  Pallas kernels: 0 us -> 181 us
  matrix products: 145 us -> 0 us
  local copies, waits for them, and re-layouts: 83.2 us -> 2.26 us
  loops' own time: 62.1 us -> 0 us
  blocking collectives: 37.6 us -> 0 us
  other arithmetic: 37.9 us -> 2.02 us
  starting transfers between devices: 32.7 us -> 0 us
  between operations: 14.5 us -> 0.02 us
    pallas_call x0 -> x1, Pallas kernels: none -> 181 us  [per_device(): pl.pallas_call(functools.partial(mega, blocks), out_shape=jax.ShapeDtypeS...]
    ppermute x8 -> x0, waiting for transfers between devices: 155 us -> none  [passed_along(): lax.ppermute(value, axis, [(source, source + steps) for source in range(i...]
    dot_general x40 -> x0, matrix products: 145 us -> none  [the longest x16 89.2 us: one_head(): lax.dot_general(query_one, key_one, (((1,), (1,)), ((), ())), preferred_e...]
    all_gather x2 -> x0, waiting for transfers between devices: 69.8 us -> none  [per_device(): lax.all_gather(normed_part, 'head', axis=1, tiled=True)]
    another operation x2 -> x0, loops' own time: 62.1 us -> none  [attend_local(): blended = lax.map(one_head, jnp.arange(local_heads, dtype=jnp.int32))]
    ppermute x8 -> x0, starting transfers between devices: 28.9 us -> none  [passed_along(): lax.ppermute(value, axis, [(source, source + steps) for source in range(i...]
    another operation x10 -> x0, local copies, waits for them, and re-layouts: 27 us -> none  [the longest x4 13.1 us: attend_local(): stacked[:, 1].reshape(key_length, local_groups, HEAD_SIZE)]
    all_to_all x1 -> x0, blocking collectives: 25.8 us -> none  [sum_at_owner(): lax.all_to_all(blocks, axis, split_axis=0, concat_axis=0, tiled=True)]
  transfers between devices with their start and end apart: 11 -> 0, of which waited for: 9 -> 0; matrix products, arithmetic and copies ran while one was open for 5% -> 0% of each run, Pallas kernels for 0% -> 0%
where the time goes in v1:
time: 186 us; the launch traced here: 185 us
  Pallas kernels  181 us (97%)
  local copies, waits for them, and re-layouts  2.26 us (1%)
  other arithmetic  2.02 us (1%)
    pallas_call x1, Pallas kernels, per_device(): pl.pallas_call(functools.partial(mega, blocks), out_shape=jax.ShapeDtypeS...  181 us

profile of v1, /device:TPU:42, one launch (start us, length us, event | category | flops | bytes accessed | tf_op | source)
XLA Modules:
  0.0 185.0 jit_solution(4381140898458597813)
XLA Ops:
  0.0 1.0 fusion
  1.0 1.0 pad_maximum_fusion
  2.0 180.7 %shard_map.73 = bf16[512,1024]{1,0:T(8,128)(2,1)} custom-call(bf16[512,1024]{1,0:T(8,128)(2,1)} %tok.1, f32[2,2048]{1,0:T(2,128)} %gain.1, bf16[2,2048,1024]{2,1,0:T(8,128)(2,1)} %wq.1, bf16[2,2048,256]{2,1,0:T(8,128)(2,1)} %wk.1, bf16[2,2048,256]{2,1,0:T(8,128)(2,1)} %wv.1, bf16[2,1024,2048]{2,1,0:T(8,128)(2,1)} %wo.1, ...), custom_call_target="tpu_custom_call" | custom-call | tf_op jit(solution)/shard_map/pallas_call | solution.py:370
  182.7 2.3 %copy.9 = bf16[512,1024]{1,0:T(8,128)(2,1)} copy(bf16[512,1024]{1,0:T(8,128)(2,1)} %shard_map.73) | data formatting | bytes 2097152
  (2 shorter events, 0.0 us)

commit v2 on v1

--- a/solution.py
+++ b/solution.py
@@ -3,6 +3,7 @@
 
 import jax
 import jax.numpy as jnp
+import numpy as np
 from jax import lax
 from jax.experimental import pallas as pl
 from jax.experimental.pallas import tpu as pltpu
@@ -26,8 +27,8 @@
 
 def mega(
     blocks,
-    tok, gain, wq, wk, wv, wo, cos_ref, sin_ref, counts, out_ref,
-    xb, wqb, wkvb, wob, nb, qs, kv, vm, m_ref, acc, ab, pb, pr, pb1, pr1,
+    tok, gain, wq, wk, wv, wo, cos_tab, sin_tab, counts, out_ref,
+    cos_ref, sin_ref, xb, wqb, wkvb, wob, nb, qs, kv, vm, m_ref, acc, ab, pb, pr, pb1, pr1,
     ld_sem, ts, tr, zs, zr, xs, xr, os_, or_, cs, cr, ps, pr_sem,
 ):
     seq = lax.axis_index("seq")
@@ -143,6 +144,16 @@
         x_copy(l, c, 1).wait_recv()
         c_copy(l, c, 1).start()
 
+    cb, sb = cos_tab[pl.ds(seq, 1), :], sin_tab[pl.ds(seq, 1), :]
+    ci, si = cos_tab[64:80, :], sin_tab[64:80, :]
+    run_cos, run_sin = cb * ci - sb * si, sb * ci + cb * si
+    cj, sj = cos_tab[80:112, :], sin_tab[80:112, :]
+    sign = jnp.where(lax.broadcasted_iota(jnp.int32, (32, HEAD_SIZE), 1) < 64, -1.0, 1.0)
+    for i in range(16):
+        a, b = run_cos[i : i + 1, :], run_sin[i : i + 1, :]
+        cos_ref[i * 32 : (i + 1) * 32, :] = a * cj - b * sj
+        sin_ref[i * 32 : (i + 1) * 32, :] = (b * cj + a * sj) * sign
+
     own_count = counts[seq]
     lanes = lax.broadcasted_iota(jnp.int32, (16, ROWS), 1)
     sub = lax.broadcasted_iota(jnp.int32, (16, ROWS), 0)
@@ -160,8 +171,8 @@
         x1 = xb[1, rows, :].astype(jnp.float32)
         total = jnp.sum(x0 * x0, axis=1, keepdims=True) + jnp.sum(x1 * x1, axis=1, keepdims=True)
         factor = lax.rsqrt(total / MODEL_WIDTH + NORM_EPSILON)
-        nb[:, 0:HALF] = (x0 * factor * gain[l : l + 1, 0:HALF]).astype(jnp.bfloat16)
-        nb[:, HALF:] = (x1 * factor * gain[l : l + 1, HALF:]).astype(jnp.bfloat16)
+        nb[:, 0:HALF] = (x0 * factor * gain[pl.ds(l, 1), 0:HALF]).astype(jnp.bfloat16)
+        nb[:, HALF:] = (x1 * factor * gain[pl.ds(l, 1), HALF:]).astype(jnp.bfloat16)
         cos = cos_ref[rows, :]
         sin = sin_ref[rows, :]
         kvp = jnp.dot(nb[...], wkvb[l], preferred_element_type=jnp.float32)
@@ -188,89 +199,71 @@
         vt = jnp.concatenate([kv[l, slot, c, 256 + g * 128 : 256 + (g + 1) * 128, :] for c in range(lo, hi)], axis=1)
         return jnp.concatenate([vt, vm[slot, :, lo * 128 : hi * 128]], axis=0)
 
-    units = [(g, c) for g in range(2) for c in range(CHUNKS)]
+    def fold(l, slot, g, c, lo, hi, s, mask, first):
+        u = g * 4 + c
+        if mask is not None:
+            key_at = lax.broadcasted_iota(jnp.int32, s.shape, 0) + lo * 128
+            row_at = (lax.broadcasted_iota(jnp.int32, s.shape, 1) & 127) + c * CHUNK
+            s = jnp.where(mask(key_at, row_at), s, LOW)
+        top = jnp.max(s, axis=0, keepdims=True)
+        if first:
+            m_new = top
+        else:
+            m_old = m_ref[u]
+            m_new = jnp.maximum(m_old, top)
+        p = jnp.exp2(s - m_new).astype(jnp.bfloat16)
+        part = jnp.dot(values_of(l, slot, g, lo, hi), p, preferred_element_type=jnp.float32)
+        m_ref[u] = m_new
+        if first:
+            acc[u] = part
+        else:
+            acc[u] = acc[u] * jnp.exp2(m_old - m_new) + part
 
     def scores(l, slot, g, c, lo, hi):
         return lax.dot_general(keys_of(l, slot, g, lo, hi), qs[g * 4 + c], NT, preferred_element_type=jnp.float32)
 
-    def sweep(l, slot, bounds, mask, first):
-        nxt_s = scores(l, slot, *units[0], *bounds(units[0][1]))
-        for n, (g, c) in enumerate(units):
+    def sweep(l, tiles, mask=None, first=False):
+        nxt_s = scores(l, *tiles[0])
+        for n, tile in enumerate(tiles):
             s = nxt_s
-            if n + 1 < len(units):
-                nxt_s = scores(l, slot, *units[n + 1], *bounds(units[n + 1][1]))
-            lo, hi = bounds(c)
-            u = g * 4 + c
-            if mask is not None:
-                key_at = lax.broadcasted_iota(jnp.int32, s.shape, 0) + lo * 128
-                row_at = (lax.broadcasted_iota(jnp.int32, s.shape, 1) & 127) + c * CHUNK
-                s = jnp.where(mask(key_at, row_at), s, LOW)
-            top = jnp.max(s, axis=0, keepdims=True)
-            if first:
-                m_new = top
-            else:
-                m_old = m_ref[u]
-                m_new = jnp.maximum(m_old, top)
-            p = jnp.exp2(s - m_new).astype(jnp.bfloat16)
-            part = jnp.dot(values_of(l, slot, g, lo, hi), p, preferred_element_type=jnp.float32)
-            m_ref[u] = m_new
-            if first:
-                acc[u] = part
-            else:
-                acc[u] = acc[u] * jnp.exp2(m_old - m_new) + part
+            if n + 1 < len(tiles):
+                nxt_s = scores(l, *tiles[n + 1])
+            fold(l, *tile, s, mask, first)
 
     def attention(l):
-        sweep(l, 0, lambda c: (0, c + 1), lambda key_at, row_at: key_at <= row_at, True)
+        every = [(g, c) for g in range(2) for c in range(CHUNKS)]
+        sweep(l, [(0, g, c, 0, c + 1) for g, c in every], lambda key_at, row_at: key_at <= row_at, True)
         event1(l, 3)
         event2(l, 2)
         event3(l, 2)
         event4(l, 1)
-
-        def step(n, carry):
-            @pl.when(n == 1)
-            def _():
-                event2(l, 3)
-                event3(l, 3)
-                event4(l, 2)
-                for c in range(CHUNKS):
-                    o_copy(l, c, 0).wait_recv()
-
-            @pl.when(n == 3)
-            def _():
-                event4(l, 3)
-                for c in range(CHUNKS):
-                    c_copy(l, c, 0).wait_recv()
-
-                @pl.when(seq >= 8)
-                def _():
-                    sweep(l, 8, lambda c: (c, 4), lambda key_at, row_at: (key_at > row_at) & (key_at < far_count), False)
-
-            @pl.when(n == 5)
-            def _():
-                for c in range(CHUNKS):
-                    o_copy(l, c, 1).wait_recv()
-
-            @pl.when(n == 6)
-            def _():
-                for c in range(CHUNKS):
-                    c_copy(l, c, 1).wait_recv()
-
-            sub_n = n % 4
-            base = 4 * (n // 4)
-            slot_lo = jnp.where(
-                n == 0, 4, jnp.where(
-                    n == 1, 3 - 2 * core, jnp.where(
-                        n == 2, 2, jnp.where(
-                            n == 3, 1 + 2 * core, jnp.where(
-                                n == 4, 6, jnp.where(n == 5, 7 - 2 * core, 5 + 2 * core))))))
-
-            @pl.when(seq >= slot_lo)
-            def _():
-                sweep(l, slot_lo, lambda c: (0, 4), None, False)
-
-            return carry
-
-        lax.fori_loop(0, 7, step, 0)
+        event2(l, 3)
+        event3(l, 3)
+
+        @pl.when(seq >= 8)
+        def _():
+            sweep(l, [(8, g, c, c, 4) for g, c in every], lambda key_at, row_at: (key_at > row_at) & (key_at < far_count))
+
+        event4(l, 2)
+        event4(l, 3)
+        for c in range(CHUNKS):
+            o_copy(l, c, 0).wait_recv()
+            c_copy(l, c, 0).wait_recv()
+            o_copy(l, c, 1).wait_recv()
+            c_copy(l, c, 1).wait_recv()
+
+    def middle(l, c):
+        @pl.when(seq >= 8)
+        def _():
+            sweep(l, [(slot, g, c, 0, 4) for slot in range(1, 8) for g in range(2)])
+
+        @pl.when(seq < 8)
+        def _():
+            def one(slot, carry):
+                sweep(l, [(slot, g, c, 0, 4) for g in range(2)])
+                return carry
+
+            lax.fori_loop(1, jnp.minimum(seq + 1, 8), one, 0)
 
     def attended(c):
         for g in range(2):
@@ -298,45 +291,68 @@
         if c >= 3:
             event4(l, c - 3)
 
-    loads[0].wait()
-    for c in range(CHUNKS):
-        tok_copy(c).wait_recv()
-        if c == 0:
-            for load in loads[1:4]:
-                load.wait()
-        project(0, c)
-        early_events(0, c)
-    attention(0)
-    loads[4].wait()
-    for c in range(CHUNKS):
-        attended(c)
-        for half in range(2):
-            pb[c, :, half * HALF : (half + 1) * HALF] = jnp.dot(
-                ab[...], wob[0, :, half * HALF : (half + 1) * HALF], preferred_element_type=jnp.float32
-            ).astype(jnp.bfloat16)
-        full_copy(c).start()
-
-    for load in loads[5:8]:
-        load.wait()
-    for c in range(CHUNKS):
-        full_copy(c).wait_recv()
-        rows = rc_rows(c)
-        for half in range(2):
-            cols = slice(half * HALF, (half + 1) * HALF)
-            summed = pb[c, :, cols].astype(jnp.float32) + pr[c, :, cols].astype(jnp.float32)
-            xb[half, rows, :] = (xb[half, rows, :].astype(jnp.float32) + summed).astype(jnp.bfloat16)
-        project(1, c)
-        early_events(1, c)
-    attention(1)
-    loads[8].wait()
     other_cols = pl.ds(pl.multiple_of(pair * HALF, HALF), HALF)
     own_cols = pl.ds(pl.multiple_of(head * HALF, HALF), HALF)
-    for c in range(CHUNKS):
-        rows = rc_rows(c)
-        attended(c)
-        pb1[c] = jnp.dot(ab[...], wob[1, :, other_cols], preferred_element_type=jnp.float32).astype(jnp.bfloat16)
-        half_copy(c).start()
-        out_ref[rows, :] = jnp.dot(ab[...], wob[1, :, own_cols], preferred_element_type=jnp.float32).astype(jnp.bfloat16)
+
+    def dots(l, cols):
+        return jnp.dot(ab[...], wob[l, :, cols], preferred_element_type=jnp.float32).astype(jnp.bfloat16)
+
+    def layer(l, carry):
+        for c in range(CHUNKS):
+            rows = rc_rows(c)
+
+            @pl.when(l == 0)
+            def _():
+                if c == 0:
+                    for load in loads[0:4]:
+                        load.wait()
+                tok_copy(c).wait_recv()
+
+            @pl.when(l == 1)
+            def _():
+                if c == 0:
+                    for load in loads[5:8]:
+                        load.wait()
+                full_copy(c).wait_recv()
+                for half in range(2):
+                    cols = slice(half * HALF, (half + 1) * HALF)
+                    summed = pb[c, :, cols].astype(jnp.float32) + pr[c, :, cols].astype(jnp.float32)
+                    xb[half, rows, :] = (xb[half, rows, :].astype(jnp.float32) + summed).astype(jnp.bfloat16)
+
+            project(l, c)
+            early_events(l, c)
+        attention(l)
+
+        @pl.when(l == 0)
+        def _():
+            loads[4].wait()
+
+        @pl.when(l == 1)
+        def _():
+            loads[8].wait()
+
+        def chunk(c, carry):
+            rows = pl.ds(pl.multiple_of(c * CHUNK, CHUNK), CHUNK)
+            middle(l, c)
+            attended(c)
+
+            @pl.when(l == 0)
+            def _():
+                for half in range(2):
+                    pb[c, :, half * HALF : (half + 1) * HALF] = dots(0, pl.ds(half * HALF, HALF))
+                full_copy(c).start()
+
+            @pl.when(l == 1)
+            def _():
+                pb1[c] = dots(1, other_cols)
+                half_copy(c).start()
+                out_ref[rows, :] = dots(1, own_cols)
+
+            return carry
+
+        return lax.fori_loop(0, CHUNKS, chunk, carry)
+
+    lax.fori_loop(0, LAYER_COUNT, layer, 0)
     for c in range(CHUNKS):
         rows = rc_rows(c)
         half_copy(c).wait_recv()
@@ -358,12 +374,11 @@
 def per_device(tokens, norm_gain, w_query, key_projection_weight, value_projection_weight, w_out, counts):
     blocks = lax.axis_size("seq")
     half_dim = HEAD_SIZE // 2
-    positions = lax.axis_index("seq") * ROWS + jnp.arange(ROWS, dtype=jnp.int32)
-    inverse = jnp.power(jnp.float32(ROPE_BASE), -2.0 * jnp.arange(half_dim, dtype=jnp.float32) / HEAD_SIZE)
-    angles = positions.astype(jnp.float32)[:, None] * inverse[None, :]
-    cosine, sine = jnp.cos(angles), jnp.sin(angles)
-    cos2 = jnp.concatenate([cosine, cosine], axis=1)
-    sin2 = jnp.concatenate([-sine, sine], axis=1)
+    inverse = ROPE_BASE ** (-2.0 * np.arange(half_dim) / HEAD_SIZE)
+    offsets = np.concatenate([np.arange(64) * ROWS, np.arange(16) * 32, np.arange(32)])
+    angles = np.tile(offsets[:, None] * inverse[None, :], (1, 2))
+    cos2 = jnp.asarray(np.cos(angles), jnp.float32)
+    sin2 = jnp.asarray(np.sin(angles), jnp.float32)
     bf16, f32 = jnp.bfloat16, jnp.float32
     any_, vmem = pl.BlockSpec(memory_space=pl.ANY), pl.BlockSpec(memory_space=pltpu.VMEM)
     dma = pltpu.SemaphoreType.DMA
@@ -373,6 +388,8 @@
         in_specs=[any_, vmem, any_, any_, any_, any_, vmem, vmem, pl.BlockSpec(memory_space=pltpu.SMEM)],
         out_specs=vmem,
         scratch_shapes=[
+            pltpu.VMEM((ROWS, HEAD_SIZE), f32),
+            pltpu.VMEM((ROWS, HEAD_SIZE), f32),
             pltpu.VMEM((2, ROWS, HALF), bf16),
             pltpu.VMEM((2, MODEL_WIDTH, HALF), bf16),
             pltpu.VMEM((2, MODEL_WIDTH, 512), bf16),

time: 186 us -> 166 us (0.89)
  Pallas kernels: 181 us -> 162 us
  other arithmetic: 2.02 us -> 0 us
    pallas_call x1, Pallas kernels: 181 us -> 162 us  [per_device(): pl.pallas_call(functools.partial(mega, blocks), out_shape=jax.ShapeDtypeS...]
where the time goes in v2:
time: 166 us; the launch traced here: 164 us
  Pallas kernels  162 us (98%)
  local copies, waits for them, and re-layouts  2.26 us (1%)
    pallas_call x1, Pallas kernels, per_device(): pl.pallas_call(functools.partial(mega, blocks), out_shape=jax.ShapeDtypeS...  162 us

profile of v2, /device:TPU:42, one launch (start us, length us, event | category | flops | bytes accessed | tf_op | source)
XLA Modules:
  0.0 164.4 jit_solution(1239798721305821564)
XLA Ops:
  0.0 162.1 %shard_map.91 = bf16[512,1024]{1,0:T(8,128)(2,1)} custom-call(bf16[512,1024]{1,0:T(8,128)(2,1)} %tok.1, f32[2,2048]{1,0:T(2,128)} %gain.1, bf16[2,2048,1024]{2,1,0:T(8,128)(2,1)} %wq.1, bf16[2,2048,256]{2,1,0:T(8,128)(2,1)} %wk.1, bf16[2,2048,256]{2,1,0:T(8,128)(2,1)} %wv.1, bf16[2,1024,2048]{2,1,0:T(8,128)(2,1)} %wo.1, f32[112,128]{1,0:T(8,128)} %constant.4.clone.cos_tab, ...), custom_call_target="tpu_custom_call" | custom-call | tf_op jit(solution)/shard_map/pallas_call | solution.py:385
  162.1 2.3 %copy.11 = bf16[512,1024]{1,0:T(8,128)(2,1)} copy(bf16[512,1024]{1,0:T(8,128)(2,1)} %shard_map.91) | data formatting | bytes 2097152

commit v3 on v2

--- a/solution.py
+++ b/solution.py
@@ -28,8 +28,8 @@
 def mega(
     blocks,
     tok, gain, wq, wk, wv, wo, cos_tab, sin_tab, counts, out_ref,
-    cos_ref, sin_ref, xb, wqb, wkvb, wob, nb, qs, kv, vm, m_ref, acc, ab, pb, pr, pb1, pr1,
-    ld_sem, ts, tr, zs, zr, xs, xr, os_, or_, cs, cr, ps, pr_sem,
+    cos_ref, sin_ref, xb, wqb, wkvb, wob, nb, qs, kv, vm, m_ref, acc, pbuf, ab, pb, pr, pb1, pr1, wot,
+    ld_sem, ts, tr, zs, zr, xs, xr, os_, or_, cs, cr, ps, pr_sem, ws, wr,
 ):
     seq = lax.axis_index("seq")
     head = lax.axis_index("head")
@@ -40,6 +40,15 @@
     xpeer = seq + 2 - 4 * xlo
     cpeer = seq + 1 - 2 * core
     pair = 1 - head
+    zi = lax.rem(lax.div(seq, 4), 4)
+    yi = lax.div(seq, 16)
+
+    def z_peer(k):
+        return seq + 4 * (lax.rem(zi + k, 4) - zi)
+
+    def y_peer(k):
+        return seq + 16 * (lax.rem(yi + k, 4) - yi)
+
     mesh_id = pl.DeviceIdType.MESH
 
     def local(src, dst, n):
@@ -58,11 +67,13 @@
         {"seq": xpeer, "head": head},
         {"seq": cpeer, "head": head},
         {"seq": seq, "head": pair},
+        *({"seq": z_peer(k), "head": head} for k in (1, 2, 3)),
+        *({"seq": y_peer(k), "head": head} for k in (1, 2, 3)),
     ):
         pl.semaphore_signal(barrier, inc=1, device_id=target, device_id_type=mesh_id)
     for load in loads:
         load.start()
-    pl.semaphore_wait(barrier, 4)
+    pl.semaphore_wait(barrier, 10)
 
     def rc_rows(c):
         return pl.ds(c * CHUNK, CHUNK)
@@ -73,8 +84,52 @@
             send_sem=ts.at[c], recv_sem=tr.at[c],
             device_id={"seq": seq, "head": pair}, device_id_type=mesh_id)
 
+    def w_copy(src, base, rows, n, target, other_head=False):
+        at = pl.ds(pl.multiple_of(base, 16), rows)
+        return pltpu.make_async_remote_copy(
+            src_ref=src.at[at, :], dst_ref=wot.at[at, :], send_sem=ws.at[n], recv_sem=wr.at[n],
+            device_id={"seq": target, "head": pair if other_head else head}, device_id_type=mesh_id)
+
+    w_base = (core * 512, core * 512 + 256)
+    w_piece = (w_base[0] + (zi * 4 + yi) * 16, w_base[1] + (yi * 4 + zi) * 16)
+    w_group = (w_base[0] + zi * 64, w_base[1] + yi * 64)
+
+    def w_pair(o):
+        return w_copy(wo.at[0], w_piece[o], 16, o, seq, True)
+
+    def w_small(o, k):
+        return w_copy(wot, w_piece[o], 16, 2 + 3 * o + k - 1, (y_peer, z_peer)[o](k))
+
+    def w_big(o, k):
+        return w_copy(wot, w_group[o], 64, 8 + 3 * o + k - 1, (z_peer, y_peer)[o](k))
+
+    def w_core():
+        return w_copy(wot, core * 512, 512, 14, cpeer)
+
+    w_all = [(o, k) for o in range(2) for k in (1, 2, 3)]
+
+    def w_event0():
+        for o in range(2):
+            w_pair(o).wait_recv()
+        for o, k in w_all:
+            w_small(o, k).start()
+
+    def w_event1():
+        for o, k in w_all:
+            w_small(o, k).wait_recv()
+        for o, k in w_all:
+            w_big(o, k).start()
+
+    def w_event2():
+        for o, k in w_all:
+            w_big(o, k).wait_recv()
+        w_core().start()
+
     for c in range(CHUNKS):
         tok_copy(c).start()
+        if c == 0:
+            w_pair(0).start()
+            w_pair(1).start()
 
     def kv_copy(l, c, src_slot, dst_slot, send, recv, stage, target):
         return pltpu.make_async_remote_copy(
@@ -199,55 +254,89 @@
         vt = jnp.concatenate([kv[l, slot, c, 256 + g * 128 : 256 + (g + 1) * 128, :] for c in range(lo, hi)], axis=1)
         return jnp.concatenate([vt, vm[slot, :, lo * 128 : hi * 128]], axis=0)
 
-    def fold(l, slot, g, c, lo, hi, s, mask, first):
-        u = g * 4 + c
-        if mask is not None:
-            key_at = lax.broadcasted_iota(jnp.int32, s.shape, 0) + lo * 128
-            row_at = (lax.broadcasted_iota(jnp.int32, s.shape, 1) & 127) + c * CHUNK
-            s = jnp.where(mask(key_at, row_at), s, LOW)
-        top = jnp.max(s, axis=0, keepdims=True)
-        if first:
-            m_new = top
-        else:
-            m_old = m_ref[u]
-            m_new = jnp.maximum(m_old, top)
-        p = jnp.exp2(s - m_new).astype(jnp.bfloat16)
-        part = jnp.dot(values_of(l, slot, g, lo, hi), p, preferred_element_type=jnp.float32)
-        m_ref[u] = m_new
-        if first:
-            acc[u] = part
-        else:
-            acc[u] = acc[u] * jnp.exp2(m_old - m_new) + part
-
     def scores(l, slot, g, c, lo, hi):
         return lax.dot_general(keys_of(l, slot, g, lo, hi), qs[g * 4 + c], NT, preferred_element_type=jnp.float32)
 
     def sweep(l, tiles, mask=None, first=False):
         nxt_s = scores(l, *tiles[0])
+        late = None
+
+        def finish(slot, g, c, lo, hi, n, fade):
+            u = g * 4 + c
+            part = jnp.dot(values_of(l, slot, g, lo, hi), pbuf[n, 0 : (hi - lo) * 128, :], preferred_element_type=jnp.float32)
+            acc[u] = part if fade is None else acc[u] * fade + part
+
         for n, tile in enumerate(tiles):
+            slot, g, c, lo, hi = tile
+            u = g * 4 + c
             s = nxt_s
             if n + 1 < len(tiles):
                 nxt_s = scores(l, *tiles[n + 1])
-            fold(l, *tile, s, mask, first)
+            if late is not None:
+                finish(*late)
+            if mask is not None:
+                key_at = lax.broadcasted_iota(jnp.int32, s.shape, 0) + lo * 128
+                row_at = (lax.broadcasted_iota(jnp.int32, s.shape, 1) & 127) + c * CHUNK
+                s = jnp.where(mask(key_at, row_at), s, LOW)
+            m_new = jnp.max(s, axis=0, keepdims=True)
+            fade = None
+            if not first:
+                m_old = m_ref[u]
+                m_new = jnp.maximum(m_old, m_new)
+                fade = jnp.exp2(m_old - m_new)
+            pbuf[n % 2, 0 : (hi - lo) * 128, :] = jnp.exp2(s - m_new).astype(jnp.bfloat16)
+            m_ref[u] = m_new
+            late = (*tile, n % 2, fade)
+        finish(*late)
+
+    every = [(g, c) for g in range(2) for c in range(CHUNKS)]
+    lane_slot = 3 - 2 * core
+    cross_slot = 1 + 2 * core
 
     def attention(l):
-        every = [(g, c) for g in range(2) for c in range(CHUNKS)]
         sweep(l, [(0, g, c, 0, c + 1) for g, c in every], lambda key_at, row_at: key_at <= row_at, True)
+
+        @pl.when(l == 1)
+        def _():
+            event1(1, 2)
+            event3(1, 1)
+
         event1(l, 3)
-        event2(l, 2)
-        event3(l, 2)
-        event4(l, 1)
+
+        def early(n, carry):
+            @pl.when(n == 0)
+            def _():
+                event2(l, 0)
+                event2(l, 1)
+                event4(l, 0)
+                event3(l, 2)
+
+            @pl.when(n == 1)
+            def _():
+                event2(l, 2)
+                event4(l, 1)
+                event3(l, 3)
+                for c in range(CHUNKS):
+                    o_copy(l, c, 0).wait_recv()
+
+            slot = jnp.where(n == 0, 4, lane_slot)
+
+            @pl.when(seq >= slot)
+            def _():
+                sweep(l, [(slot, g, c, 0, 4) for g, c in every])
+
+            return carry
+
+        lax.fori_loop(0, 2, early, 0)
         event2(l, 3)
-        event3(l, 3)
+        event4(l, 2)
 
         @pl.when(seq >= 8)
         def _():
             sweep(l, [(8, g, c, c, 4) for g, c in every], lambda key_at, row_at: (key_at > row_at) & (key_at < far_count))
 
-        event4(l, 2)
         event4(l, 3)
         for c in range(CHUNKS):
-            o_copy(l, c, 0).wait_recv()
             c_copy(l, c, 0).wait_recv()
             o_copy(l, c, 1).wait_recv()
             c_copy(l, c, 1).wait_recv()
@@ -255,26 +344,31 @@
     def middle(l, c):
         @pl.when(seq >= 8)
         def _():
-            sweep(l, [(slot, g, c, 0, 4) for slot in range(1, 8) for g in range(2)])
+            sweep(l, [(slot, g, c, 0, 4) for slot in (cross_slot, 2, 5, 6, 7) for g in range(2)])
 
         @pl.when(seq < 8)
         def _():
-            def one(slot, carry):
-                sweep(l, [(slot, g, c, 0, 4) for g in range(2)])
+            def one(n, carry):
+                slot = jnp.where(n == 0, cross_slot, jnp.where(n == 1, 2, n + 3))
+
+                @pl.when(seq >= slot)
+                def _():
+                    sweep(l, [(slot, g, c, 0, 4) for g in range(2)])
+
                 return carry
 
-            lax.fori_loop(1, jnp.minimum(seq + 1, 8), one, 0)
+            lax.fori_loop(0, 5, one, 0)
 
     def attended(c):
         for g in range(2):
             u = g * 4 + c
             norm = acc[u, 0:128, :] / acc[u, 128:129, :]
             for h in range(4):
-                ab[:, (g * 4 + h) * 128 : (g * 4 + h + 1) * 128] = norm[:, h * 128 : (h + 1) * 128].T.astype(jnp.bfloat16)
+                ab[c, :, (g * 4 + h) * 128 : (g * 4 + h + 1) * 128] = norm[:, h * 128 : (h + 1) * 128].T.astype(jnp.bfloat16)
 
     def full_copy(c):
         return pltpu.make_async_remote_copy(
-            src_ref=pb.at[c], dst_ref=pr.at[c], send_sem=ps.at[0, c], recv_sem=pr_sem.at[0, c],
+            src_ref=ab.at[c], dst_ref=pr.at[c], send_sem=ps.at[0, c], recv_sem=pr_sem.at[0, c],
             device_id={"seq": seq, "head": pair}, device_id_type=mesh_id)
 
     def half_copy(c):
@@ -283,19 +377,28 @@
             device_id={"seq": seq, "head": pair}, device_id_type=mesh_id)
 
     def early_events(l, c):
-        if c >= 1:
-            event1(l, c - 1)
-        if c >= 2:
-            event2(l, c - 2)
-            event3(l, c - 2)
-        if c >= 3:
-            event4(l, c - 3)
+        @pl.when(l == 0)
+        def _():
+            if c >= 1:
+                event1(0, c - 1)
+            if c >= 2:
+                event3(0, c - 2)
+            if c == 1:
+                w_event0()
+
+        @pl.when(l == 1)
+        def _():
+            if c == 2:
+                event1(1, 0)
+            if c == 3:
+                event1(1, 1)
+                event3(1, 0)
 
     other_cols = pl.ds(pl.multiple_of(pair * HALF, HALF), HALF)
     own_cols = pl.ds(pl.multiple_of(head * HALF, HALF), HALF)
 
-    def dots(l, cols):
-        return jnp.dot(ab[...], wob[l, :, cols], preferred_element_type=jnp.float32).astype(jnp.bfloat16)
+    def dots(l, c, cols):
+        return jnp.dot(ab[c], wob[l, :, cols], preferred_element_type=jnp.float32).astype(jnp.bfloat16)
 
     def layer(l, carry):
         for c in range(CHUNKS):
@@ -313,10 +416,12 @@
                 if c == 0:
                     for load in loads[5:8]:
                         load.wait()
+                    w_core().wait_recv()
                 full_copy(c).wait_recv()
                 for half in range(2):
                     cols = slice(half * HALF, (half + 1) * HALF)
-                    summed = pb[c, :, cols].astype(jnp.float32) + pr[c, :, cols].astype(jnp.float32)
+                    arrived = jnp.dot(pr[c], wot[:, cols], preferred_element_type=jnp.float32).astype(jnp.bfloat16)
+                    summed = pb[c, :, cols].astype(jnp.float32) + arrived.astype(jnp.float32)
                     xb[half, rows, :] = (xb[half, rows, :].astype(jnp.float32) + summed).astype(jnp.bfloat16)
 
             project(l, c)
@@ -325,6 +430,7 @@
 
         @pl.when(l == 0)
         def _():
+            w_event1()
             loads[4].wait()
 
         @pl.when(l == 1)
@@ -334,19 +440,28 @@
         def chunk(c, carry):
             rows = pl.ds(pl.multiple_of(c * CHUNK, CHUNK), CHUNK)
             middle(l, c)
+
+            @pl.when(l == 1)
+            def _():
+                full_copy(c).wait_send()
+
             attended(c)
 
             @pl.when(l == 0)
             def _():
+                full_copy(c).start()
                 for half in range(2):
-                    pb[c, :, half * HALF : (half + 1) * HALF] = dots(0, pl.ds(half * HALF, HALF))
-                full_copy(c).start()
+                    pb[c, :, half * HALF : (half + 1) * HALF] = dots(0, c, pl.ds(half * HALF, HALF))
+
+                @pl.when(c == 2)
+                def _():
+                    w_event2()
 
             @pl.when(l == 1)
             def _():
-                pb1[c] = dots(1, other_cols)
+                pb1[c] = dots(1, c, other_cols)
                 half_copy(c).start()
-                out_ref[rows, :] = dots(1, own_cols)
+                out_ref[rows, :] = dots(1, c, own_cols)
 
             return carry
 
@@ -359,9 +474,14 @@
         summed = out_ref[rows, :].astype(jnp.float32) + pr1[c].astype(jnp.float32)
         out_ref[rows, :] = (xb[head, rows, :].astype(jnp.float32) + summed).astype(jnp.bfloat16)
 
+    w_pair(0).wait_send()
+    w_pair(1).wait_send()
+    w_core().wait_send()
+    for o, k in w_all:
+        w_small(o, k).wait_send()
+        w_big(o, k).wait_send()
     for c in range(CHUNKS):
         tok_copy(c).wait_send()
-        full_copy(c).wait_send()
         half_copy(c).wait_send()
         for l in range(LAYER_COUNT):
             for i in range(2):
@@ -400,15 +520,17 @@
             pltpu.VMEM((SLOTS, 16, ROWS), bf16),
             pltpu.VMEM((8, 1, 512), f32),
             pltpu.VMEM((8, 144, 512), f32),
-            pltpu.VMEM((CHUNK, HALF), bf16),
-            pltpu.VMEM((CHUNKS, CHUNK, MODEL_WIDTH), bf16),
+            pltpu.VMEM((2, ROWS, 512), bf16),
+            pltpu.VMEM((CHUNKS, CHUNK, HALF), bf16),
             pltpu.VMEM((CHUNKS, CHUNK, MODEL_WIDTH), bf16),
             pltpu.VMEM((CHUNKS, CHUNK, HALF), bf16),
             pltpu.VMEM((CHUNKS, CHUNK, HALF), bf16),
+            pltpu.VMEM((CHUNKS, CHUNK, HALF), bf16),
+            pltpu.VMEM((HALF, MODEL_WIDTH), bf16),
             dma((9,)), dma((4,)), dma((4,)),
             dma((2, 2, 4)), dma((2, 2, 4)), dma((2, 2, 4)), dma((2, 2, 4)),
             dma((2, 2, 4)), dma((2, 2, 4)), dma((2, 2, 4)), dma((2, 2, 4)),
-            dma((2, 4)), dma((2, 4)),
+            dma((2, 4)), dma((2, 4)), dma((15,)), dma((15,)),
         ],
         compiler_params=pltpu.CompilerParams(
             collective_id=0, has_side_effects=True, vmem_limit_bytes=63 * 2**20

time: 166 us -> 147 us (0.89)
  the two profiles are of different devices: /device:TPU:42 before, /device:TPU:9 now
where the time goes in v3:
time: 147 us
  Pallas kernels  145 us (99%)
  local copies, waits for them, and re-layouts  2.26 us (2%)
    pallas_call x1, Pallas kernels, per_device(): pl.pallas_call(functools.partial(mega, blocks), out_shape=jax.ShapeDtypeS...  145 us

profile of v3, /device:TPU:9, one launch (start us, length us, event | category | flops | bytes accessed | tf_op | source)
XLA Modules:
  0.0 147.0 jit_solution(6279044198924457474)
XLA Ops:
  0.0 144.7 %shard_map.91 = bf16[512,1024]{1,0:T(8,128)(2,1)} custom-call(bf16[512,1024]{1,0:T(8,128)(2,1)} %tok.1, f32[2,2048]{1,0:T(2,128)} %gain.1, bf16[2,2048,1024]{2,1,0:T(8,128)(2,1)} %wq.1, bf16[2,2048,256]{2,1,0:T(8,128)(2,1)} %wk.1, bf16[2,2048,256]{2,1,0:T(8,128)(2,1)} %wv.1, bf16[2,1024,2048]{2,1,0:T(8,128)(2,1)} %wo.1, f32[112,128]{1,0:T(8,128)} %constant.4.clone.cos_tab, ...), custom_call_target="tpu_custom_call" | custom-call | tf_op jit(solution)/shard_map/pallas_call | solution.py:505
  144.7 2.3 %copy.11 = bf16[512,1024]{1,0:T(8,128)(2,1)} copy(bf16[512,1024]{1,0:T(8,128)(2,1)} %shard_map.91) | data formatting | bytes 2097152
